TPU v7x, 32 devices: a whole 2x2x4 slice. The times are simulated.
32 devices in a mesh: patch: 16 (over z, y, core), chan: 2 (over x).
Axes of the slice: x: 2, y: 2, z: 4, core: 2. Of those that a mesh axis runs over, the one named last changes fastest.
Arguments:
- tokens: bfloat16 [1, 8192, 1280], P(None, 'patch'), may hold values from -12 to 12
- stale_k: bfloat16 [1, 8192, 1024], P(None, 'patch', 'chan'), may hold values from -64 to 64
- stale_v: bfloat16 [1, 8192, 1024], P(None, 'patch', 'chan'), may hold values from -6 to 6
- w_query: bfloat16 [1280, 1024], P(None, 'chan'), may hold values from -0.15625 to 0.15625
- w_key: bfloat16 [1280, 1024], P(None, 'chan'), may hold values from -0.4375 to 0.4375
- w_value: bfloat16 [1280, 1024], P(None, 'chan'), may hold values from -0.15625 to 0.15625
- w_out: bfloat16 [1024, 1280], P('chan'), may hold values from -0.1875 to 0.1875
- ff_value: bfloat16 [1280, 5120], P(None, 'chan'), may hold values from -0.15625 to 0.15625
- ff_gate: bfloat16 [1280, 5120], P(None, 'chan'), may hold values from -0.15625 to 0.15625
- ff_down: bfloat16 [5120, 1280], P('chan'), may hold values from -0.078125 to 0.078125
Outputs:
- layer_out: bfloat16 [1, 8192, 1280], P(None, 'patch', 'chan')
All inputs are finite; a program needn't handle non-finite values.
Results may differ from a plain program's by a relative error of at most 0.0095.
Values may be sent and summed in bfloat16 or wider, within the bound.
No kernel may reach another device: no remote copies, remote signals or barrier semaphores. Data moves between devices by JAX's collectives and lax.ppermute only.
A program may use at most 128 MiB of HBM per device.

v0:
```python
import functools

import jax
import jax.numpy as jnp
from jax import lax
from jax.experimental import pallas as pl
from jax.experimental.pallas import tpu as pltpu
from jax.sharding import PartitionSpec as P


HD = 64
LANES = 128


def dot_nt(a, b):
    return lax.dot_general(a, b, (((1,), (1,)), ((), ())), preferred_element_type=jnp.float32)


def dot_nn(a, b):
    return jnp.dot(a, b, preferred_element_type=jnp.float32)


def swap(x):
    return jnp.concatenate([x[:, HD:], x[:, :HD]], axis=1)


def low_half(shape):
    return lax.broadcasted_iota(jnp.int32, shape, 1) < HD


def layer_norm(values):
    mean = jnp.mean(values, axis=-1, keepdims=True)
    centered = values - mean
    var = jnp.mean(centered * centered, axis=-1, keepdims=True)
    return centered * lax.rsqrt(var + 1e-05)


def whole(shape):
    return pl.BlockSpec(shape, lambda *_: (0,) * len(shape))


def params(mib, **more):
    return pltpu.CompilerParams(vmem_limit_bytes=mib * 2**20, **more)


def cost(flops, moved, trans=0):
    return pl.CostEstimate(flops=int(flops), bytes_accessed=int(moved), transcendentals=int(trans))


STAT_ROWS = 16


def write_result(out_ref, start, parts, with_stats):
    rows = parts[0][0].shape[0]
    low = low_half((rows, LANES))
    sides = [accum / swap(accum) for accum, _ in parts]
    out_ref[start : start + rows, :] = jnp.where(low, swap(sides[0]), sides[1]).astype(
        jnp.bfloat16
    )
    if not with_stats:
        return
    lane = lax.broadcasted_iota(jnp.int32, (rows, LANES), 1)
    table = jnp.zeros((rows, LANES), jnp.float32)
    for side, (accum, top) in enumerate(parts):
        rest = jnp.where(low, top + jnp.log(jnp.where(low, accum, 1.0)), 0.0)
        for part in range(3):
            piece = rest.astype(jnp.bfloat16).astype(jnp.float32)
            rest = rest - piece
            table = jnp.where(lane == 3 * side + part, piece, table)
    pick_shape = (STAT_ROWS, LANES)
    pick = lax.broadcasted_iota(jnp.int32, pick_shape, 0) == lax.broadcasted_iota(
        jnp.int32, pick_shape, 1
    )
    stats = dot_nt(
        jnp.where(pick, 1.0, 0.0).astype(jnp.bfloat16), table.astype(jnp.bfloat16)
    ).astype(jnp.bfloat16)
    for at in range(rows // LANES):
        first = start + rows + at * STAT_ROWS
        out_ref[first : first + STAT_ROWS, :] = stats[:, at * LANES : (at + 1) * LANES]


def result_rows(rows):
    return rows + rows // LANES * STAT_ROWS


def read_stats(ref, start, rows):
    stats = jnp.concatenate(
        [
            ref[start + rows + at * STAT_ROWS : start + rows + (at + 1) * STAT_ROWS, :]
            for at in range(rows // LANES)
        ],
        axis=1,
    )
    row = lax.broadcasted_iota(jnp.int32, (STAT_ROWS, LANES), 0)
    low = low_half((STAT_ROWS, LANES))
    spread = jnp.where((row < 3) & low | (row >= 3) & (row < 6) & ~low, 1.0, 0.0)
    return lax.dot_general(
        stats,
        spread.astype(jnp.bfloat16),
        (((0,), (0,)), ((), ())),
        preferred_element_type=jnp.float32,
    )


def merge_results(ref, start, local_ref, local_start, rows):
    one = ref[start : start + rows, :].astype(jnp.float32)
    two = local_ref[local_start : local_start + rows, :].astype(jnp.float32)
    gap = read_stats(local_ref, local_start, rows) - read_stats(ref, start, rows)
    share = 1.0 / (1.0 + jnp.exp(gap))
    return (two + (one - two) * share).astype(jnp.bfloat16)


def local_kernel(count, *refs):
    q_refs, fresh_refs = refs[:count], refs[count : 2 * count]
    out_ref, packed_ref, fresh_ref = refs[2 * count :]
    for at in range(count):

        @pl.when(pl.program_id(0) == at)
        def _(at=at):
            packed_ref[...] = q_refs[at][...]
            fresh_ref[...] = fresh_refs[at][...]

    packed, fresh = packed_ref[...], fresh_ref[...]
    low = low_half(packed.shape)
    fresh_v = jnp.where(low_half(fresh.shape), jnp.ones_like(fresh), fresh)
    zero = jnp.zeros_like(packed)
    parts = []
    for query in (jnp.where(low, packed, zero), jnp.where(low, swap(packed), zero)):
        scores = dot_nt(query, fresh)
        top = jnp.max(scores, axis=1, keepdims=True)
        parts.append((dot_nn(jnp.exp(scores - top).astype(jnp.bfloat16), fresh_v), top))
    write_result(out_ref, 0, parts, True)


def attend_local(queries, fresh):
    count, rows = len(queries), queries[0].shape[0]
    size = result_rows(rows)
    return pl.pallas_call(
        functools.partial(local_kernel, count),
        grid=(count,),
        in_specs=[whole(value.shape) for value in (*queries, *fresh)],
        out_specs=pl.BlockSpec((size, LANES), lambda i: (i, 0)),
        out_shape=jax.ShapeDtypeStruct((count * size, LANES), jnp.bfloat16),
        scratch_shapes=[
            pltpu.VMEM(queries[0].shape, jnp.bfloat16),
            pltpu.VMEM(fresh[0].shape, jnp.bfloat16),
        ],
        compiler_params=params(16, dimension_semantics=("arbitrary",)),
        cost_estimate=cost(16 * count * rows * rows * LANES, 8 * count * rows * LANES),
        name="attend_local",
    )(*queries, *fresh)


def head_tile(ref, head):
    return ref[:, pl.ds(pl.multiple_of((head // 2) * LANES, LANES), LANES)]


def pack_kv(member, step, k_ref, v_ref, store):
    head = jnp.bitwise_xor(member, step)

    def put(odd):
        k_tile, v_tile = head_tile(k_ref, head), head_tile(v_ref, head)
        low = low_half(k_tile.shape)
        store(jnp.where(low, swap(k_tile), v_tile) if odd else jnp.where(low, k_tile, swap(v_tile)))

    pl.when(head % 2 == 0)(lambda: put(False))
    pl.when(head % 2 == 1)(lambda: put(True))


def pack_kernel(steps, member_ref, k_ref, v_ref, *out_refs):
    for step, out in zip(steps, out_refs):

        def store(value, out=out):
            out[...] = value

        pack_kv(member_ref[0], step, k_ref, v_ref, store)


def pack_stale(member, stale_k, stale_v, steps):
    rows, width = stale_k.shape
    packet = jax.ShapeDtypeStruct((rows, LANES), jnp.bfloat16)
    return pl.pallas_call(
        functools.partial(pack_kernel, steps),
        in_specs=[
            pl.BlockSpec(memory_space=pltpu.SMEM),
            pl.BlockSpec(memory_space=pltpu.VMEM),
            pl.BlockSpec(memory_space=pltpu.VMEM),
        ],
        out_specs=[pl.BlockSpec(memory_space=pltpu.VMEM)] * len(steps),
        out_shape=[packet] * len(steps),
        compiler_params=params(8),
        cost_estimate=cost(1e9, 4 * rows * width * 2),
        name="pack_stale",
    )(member, stale_k, stale_v)


def qkv_kernel(near, group, member_ref, x_ref, k_ref, v_ref, wq_hbm, wk_hbm, wv_hbm, *rest):
    out_refs, rest = rest[:group], rest[group:]
    fresh_refs, (wq, wk, wv, qs, ks, vs, sems) = rest[: group - near], rest[group - near :]
    copies = [
        pltpu.make_async_copy(src, dst, sems.at[at])
        for at, (src, dst) in enumerate(((wq_hbm, wq), (wk_hbm, wk), (wv_hbm, wv)))
    ]
    for copy in copies:
        copy.start()
    rows = x_ref.shape[0]
    half = rows // 2
    member = member_ref[0]
    for step in range(near):

        def store_stale(value, out=out_refs[step]):
            out[half + rows :, :] = value

        pack_kv(member, step, k_ref, v_ref, store_stale)
    normed = layer_norm(x_ref[...].astype(jnp.float32)).astype(jnp.bfloat16)
    copies[0].wait()
    qs[...] = (dot_nn(normed, wq[...]).astype(jnp.bfloat16) * (1.0 / HD**0.5)).astype(jnp.bfloat16)
    copies[1].wait()
    ks[...] = dot_nn(normed, wk[...]).astype(jnp.bfloat16)
    copies[2].wait()
    vs[...] = dot_nn(normed, wv[...]).astype(jnp.bfloat16)
    for step in range(group):
        out = out_refs[step]
        head = jnp.bitwise_xor(member, step)

        def put(odd, out=out, head=head):
            tile = head_tile(qs, head)
            low = low_half((half, LANES))
            first, second = tile[:half], tile[half:]
            if odd:
                out[:half, :] = jnp.where(low, swap(first), second)
            else:
                out[:half, :] = jnp.where(low, first, swap(second))

        pl.when(head % 2 == 0)(functools.partial(put, False))
        pl.when(head % 2 == 1)(functools.partial(put, True))

        def store(value, out=out, step=step):
            if step < near:
                out[half : half + rows, :] = value
            else:
                fresh_refs[step - near][...] = value

        pack_kv(member, step, ks, vs, store)


def project_qkv(member, tokens, stale_k, stale_v, w_query, w_key, w_value, near, group):
    rows, width = tokens.shape
    out_width = w_query.shape[1]
    return pl.pallas_call(
        functools.partial(qkv_kernel, near, group),
        in_specs=[pl.BlockSpec(memory_space=pltpu.SMEM)]
        + [pl.BlockSpec(memory_space=pltpu.VMEM)] * 3
        + [pl.BlockSpec(memory_space=pltpu.HBM)] * 3,
        out_specs=[pl.BlockSpec(memory_space=pltpu.VMEM)] * (2 * group - near),
        out_shape=[
            jax.ShapeDtypeStruct((size, LANES), jnp.bfloat16)
            for size in [rows // 2 + 2 * rows] * near
            + [rows // 2] * (group - near)
            + [rows] * (group - near)
        ],
        scratch_shapes=[pltpu.VMEM((width, out_width), jnp.bfloat16)] * 3
        + [pltpu.VMEM((rows, out_width), jnp.bfloat16)] * 3
        + [pltpu.SemaphoreType.DMA((3,))],
        compiler_params=params(60),
        cost_estimate=cost(6 * rows * width * out_width, 2 * 3 * width * out_width),
        name="project_qkv",
    )(member, tokens, stale_k, stale_v, w_query, w_key, w_value)


def attend_kernel(plan, *refs):
    count, blocks, queries, kv_rows = plan["count"], plan["blocks"], plan["queries"], plan["rows"]
    arrays, refs = refs[: plan["arrays"]], refs[plan["arrays"] :]
    state_in, refs = (refs[:1], refs[1:]) if plan["resume"] else (None, refs)
    outs = 1 if plan["partial"] else count
    out_refs, (kvs, ones_v, qfs, result) = refs[:outs], refs[outs:]
    at = pl.program_id(0)
    half = kv_rows // 2
    low_kv = low_half((kv_rows, LANES))
    low_q = low_half((half, LANES))
    q_rows = qfs.shape[1]

    @pl.when(at == 0)
    def _():
        for b, (ref, start) in enumerate(blocks):
            block = arrays[ref][start : start + kv_rows, :]
            kvs[b] = block
            ones_v[b] = jnp.where(low_kv, jnp.ones_like(block), block)
        for i, ref in enumerate(queries):
            qfs[i] = arrays[ref][:q_rows, :]

    packed = qfs[at, :half, :]
    zero = jnp.zeros_like(packed)
    if plan["own"] is None:
        keys = [(kvs, ones_v, b) for b in range(len(blocks))]
    else:
        own = plan["own"] + at
        keys = [
            (kvs, ones_v, b + (b >= own).astype(jnp.int32)) for b in range(len(blocks) - 1)
        ]
    fresh, fresh_v = None, None
    if plan["fresh"]:
        fresh = qfs[at, half:, :]
        fresh_v = jnp.where(low_kv, jnp.ones_like(fresh), fresh)
    results = []
    for side, query in enumerate(
        (jnp.where(low_q, packed, zero), jnp.where(low_q, swap(packed), zero))
    ):
        scores = [dot_nt(query, ref[pick]) for ref, _, pick in keys]
        if fresh is not None:
            scores.append(dot_nt(query, fresh))
        top = scores[0]
        for block in scores[1:]:
            top = jnp.maximum(top, block)
        top = jnp.max(top, axis=1, keepdims=True)
        accum = None
        for b, block in enumerate(scores):
            weights = jnp.exp(block - top).astype(jnp.bfloat16)
            part = dot_nn(weights, keys[b][1][keys[b][2]] if b < len(keys) else fresh_v)
            accum = part if accum is None else accum + part
        if plan["resume"]:
            carried = state_in[0][0, side]
            top_in = carried[:, :1]
            accum_in = jnp.where(low_q, carried[:, HD - 1 : HD], carried)
            both = jnp.maximum(top_in, top)
            accum = accum_in * jnp.exp(top_in - both) + accum * jnp.exp(top - both)
        if plan["partial"]:
            lane = lax.broadcasted_iota(jnp.int32, (half, LANES), 1)
            out_refs[0][0, side] = jnp.where(lane < HD // 2, top, accum)
        else:
            results.append((accum, top))
    if not plan["partial"]:
        write_result(result, 0, results, plan["stats"])
        for i in range(count):

            @pl.when(at == i)
            def _(i=i):
                out_refs[i][...] = result[: out_refs[i].shape[0], :]


def attend(queries, kv_blocks, kv_rows, own, fresh, state=None, partial=False, stats=False):
    arrays = []

    def place(value):
        for at, known in enumerate(arrays):
            if known is value:
                return at
        arrays.append(value)
        return len(arrays) - 1

    count = len(queries)
    half = kv_rows // 2
    plan = {
        "count": count,
        "queries": [place(query) for query in queries],
        "blocks": [(place(value), start) for value, start in kv_blocks],
        "rows": kv_rows,
        "own": own,
        "resume": state is not None,
        "partial": partial,
        "fresh": fresh,
        "stats": stats,
    }
    plan["arrays"] = len(arrays)
    blocks = len(kv_blocks)
    pairs = count * 2 * half * blocks * kv_rows
    carried = pl.BlockSpec((1, 2, half, LANES), lambda i: (i, 0, 0, 0))
    if partial:
        out_specs = [carried]
        out_shape = [jax.ShapeDtypeStruct((count, 2, half, LANES), jnp.float32)]
    else:
        packet = (result_rows(half) if stats else half, LANES)
        out_specs = [whole(packet)] * count
        out_shape = [jax.ShapeDtypeStruct(packet, jnp.bfloat16)] * count
    return pl.pallas_call(
        functools.partial(attend_kernel, plan),
        grid=(count,),
        in_specs=[whole(value.shape) for value in arrays] + ([carried] if state else []),
        out_specs=out_specs,
        out_shape=out_shape,
        scratch_shapes=[
            pltpu.VMEM((blocks, kv_rows, LANES), jnp.bfloat16),
            pltpu.VMEM((blocks, kv_rows, LANES), jnp.bfloat16),
            pltpu.VMEM((count, half + kv_rows if fresh else half, LANES), jnp.bfloat16),
            pltpu.VMEM((result_rows(half), LANES), jnp.bfloat16),
        ],
        compiler_params=params(4 + blocks * kv_rows // 186, dimension_semantics=("arbitrary",)),
        cost_estimate=cost(4 * pairs * LANES, 2 * blocks * kv_rows * LANES, pairs),
    )(*arrays, *(state or ()))


def ffn_kernel(spots, counts, aligned, scalars_ref, tokens_ref, *refs):
    arrays, chans = counts
    packets, refs = refs[:arrays], refs[arrays:]
    w_out_refs, refs = refs[:chans], refs[chans:]
    val_ref, gate_ref, down_hbm, resid_ref, gated_ref, part_ref, *refs = refs
    heads, normed_two, gated_all, down, sem = refs
    rows = tokens_ref.shape[0]
    half = rows // 2
    at, last = pl.program_id(0), pl.num_programs(0) - 1
    share = part_ref.shape[1]
    member, target, chan = scalars_ref[0], scalars_ref[1], scalars_ref[2]

    def columns(index, size):
        return pl.ds(pl.multiple_of(index * size, LANES), size)

    down_src = down_hbm.at[:, columns(target, share)] if aligned else down_hbm
    down_copy = pltpu.make_async_copy(down_src, down, sem)

    @pl.when(at == 0)
    def _():
        down_copy.start()
        low = low_half((half, LANES))
        for c in range(chans):
            for pair in range(len(spots[c]) // 2):
                place = columns(jnp.bitwise_xor(member // 2, pair), LANES)

                def put(odd, pair=pair, place=place, c=c):
                    one, two = (
                        packets[ref][start : start + half, :]
                        if local is None
                        else merge_results(packets[ref], start, packets[local], local_start, half)
                        for ref, start, local, local_start in spots[c][2 * pair : 2 * pair + 2]
                    )
                    even_head, odd_head = (two, one) if odd else (one, two)
                    heads[c, :half, place] = jnp.where(low, even_head, swap(odd_head))
                    heads[c, half:, place] = jnp.where(low, swap(even_head), odd_head)

                pl.when(member % 2 == 0)(functools.partial(put, False))
                pl.when(member % 2 == 1)(functools.partial(put, True))
        resid = tokens_ref[...].astype(jnp.float32)
        for c in range(chans):
            resid = resid + dot_nn(heads[c], w_out_refs[c][...])
        if aligned:
            for c in range(chans):

                @pl.when(chan == c)
                def _(c=c):
                    resid_ref[...] = resid[:, c * share : (c + 1) * share]
        else:
            resid_ref[...] = resid
        normed_two[...] = layer_norm(resid).astype(jnp.bfloat16)

    block = gated_ref.shape[1]
    piece = 256 if block % 256 == 0 else block
    for start in range(0, block, piece):
        ff_val = dot_nn(normed_two[...], val_ref[:, start : start + piece])
        gate = dot_nn(normed_two[...], gate_ref[:, start : start + piece])
        gelu = 0.5 * gate * (1.0 + lax.erf(gate * (0.5**0.5)))
        gated = (ff_val * gelu).astype(jnp.bfloat16)
        gated_ref[:, start : start + piece] = gated
        gated_all[:, pl.ds(pl.multiple_of(at * block + start, LANES), piece)] = gated

    @pl.when(at == last)
    def _():
        down_copy.wait()
        part_ref[...] = dot_nn(gated_all[...], down[...]).astype(part_ref.dtype)


def out_and_ffn(scalars, tokens, packets, w_outs, ff_value, ff_gate, ff_down, share):
    rows, width = tokens.shape
    hidden = ff_value.shape[1]
    block = next(size for size in (512, 256, 128) if hidden % size == 0)
    chans = len(w_outs)
    heads_width = w_outs[0].shape[0]
    arrays, spots = [], []

    def place(value):
        if value is None:
            return None
        for at, known in enumerate(arrays):
            if known is value:
                return at
        arrays.append(value)
        return len(arrays) - 1

    for chan in packets:
        spots.append([])
        for value, start, local, local_start in chan:
            spots[-1].append((place(value), start, place(local), local_start))
    aligned = share % LANES == 0
    if not aligned:
        ff_down = lax.dynamic_slice_in_dim(ff_down, scalars[1] * share, share, 1)
    return pl.pallas_call(
        functools.partial(ffn_kernel, spots, (len(arrays), chans), aligned),
        grid=(hidden // block,),
        in_specs=[pl.BlockSpec(memory_space=pltpu.SMEM), whole(tokens.shape)]
        + [whole(value.shape) for value in arrays]
        + [whole(w.shape) for w in w_outs]
        + [pl.BlockSpec((width, block), lambda i: (0, i))] * 2
        + [pl.BlockSpec(memory_space=pltpu.HBM)],
        out_specs=[
            whole((rows, share if aligned else width)),
            pl.BlockSpec((rows, block), lambda i: (0, i)),
            whole((rows, share)),
        ],
        out_shape=[
            jax.ShapeDtypeStruct((rows, share if aligned else width), jnp.float32),
            jax.ShapeDtypeStruct((rows, hidden), jnp.bfloat16),
            jax.ShapeDtypeStruct((rows, share), jnp.bfloat16),
        ],
        scratch_shapes=[
            pltpu.VMEM((chans, rows, heads_width), jnp.bfloat16),
            pltpu.VMEM((rows, width), jnp.bfloat16),
            pltpu.VMEM((rows, hidden), jnp.bfloat16),
            pltpu.VMEM((hidden, share), jnp.bfloat16),
            pltpu.SemaphoreType.DMA,
        ],
        compiler_params=params(40, dimension_semantics=("arbitrary",)),
        cost_estimate=cost(4 * rows * width * hidden, 4 * width * hidden, rows * hidden),
        name="out_and_ffn",
    )(scalars, tokens, *arrays, *w_outs, ff_value, ff_gate, ff_down)


def down_kernel(target_ref, gated_ref, down_ref, out_ref, total):
    at = pl.program_id(0)
    part = dot_nn(gated_ref[...], down_ref[...])

    @pl.when(at == 0)
    def _():
        total[...] = part

    @pl.when(at > 0)
    def _():
        total[...] += part

    @pl.when(at == pl.num_programs(0) - 1)
    def _():
        out_ref[...] = total[...].astype(out_ref.dtype)


def down_project(target, gated, ff_down, share, dtype):
    rows, hidden = gated.shape
    if share % LANES != 0:
        ff_down = lax.dynamic_slice_in_dim(ff_down, target * share, share, 1)
        target = jnp.zeros_like(target)
    block = next(size for size in (1280, 640, 512, 256, 128, hidden) if hidden % size == 0)
    return pl.pallas_call(
        down_kernel,
        grid_spec=pltpu.PrefetchScalarGridSpec(
            num_scalar_prefetch=1,
            grid=(hidden // block,),
            in_specs=[
                pl.BlockSpec((rows, block), lambda k, target: (0, k)),
                pl.BlockSpec((block, share), lambda k, target: (k, target[0])),
            ],
            out_specs=pl.BlockSpec((rows, share), lambda k, target: (0, 0)),
            scratch_shapes=[pltpu.VMEM((rows, share), jnp.float32)],
        ),
        out_shape=jax.ShapeDtypeStruct((rows, share), dtype),
        compiler_params=params(20, dimension_semantics=("arbitrary",)),
        cost_estimate=cost(2 * rows * hidden * share, 2 * hidden * share),
        name="down_project",
    )(target.reshape(1), gated, ff_down)


def image_block(
    tokens, stale_k, stale_v, w_query, w_key, w_value, w_outs, ff_value, ff_gate, ff_down
):
    rows, width = tokens.shape
    head_count = w_query.shape[1] // HD
    patches = lax.axis_size("patch")
    chans = lax.axis_size("chan")
    group = 1
    while head_count % (2 * group) == 0 and patches % (2 * group) == 0:
        group *= 2
    assert group == head_count and group >= 2
    near = group // 2
    peers = patches // group
    patch_id = lax.axis_index("patch")
    chan_id = lax.axis_index("chan").astype(jnp.int32)
    member = (patch_id // peers).astype(jnp.int32).reshape(1)

    def partner(p, step):
        return ((p // peers) ^ step) * peers + p % peers

    def trade(value, step):
        if step == 0:
            return value
        return lax.ppermute(value, "patch", [(p, partner(p, step)) for p in range(patches)])

    def beside(value, step):
        pairs = [
            (p, p // peers * peers + (p % peers + step) % peers) for p in range(patches)
        ]
        return lax.ppermute(value, "patch", pairs)

    def over_chan(value, step):
        return lax.ppermute(value, "chan", [(c, (c + step) % chans) for c in range(chans)])

    def trade_over_chan(value, step, chan_step):
        if chan_step == 0:
            return trade(value, step)
        pairs = [
            (p * chans + c, partner(p, step) * chans + (c + chan_step) % chans)
            for p in range(patches)
            for c in range(chans)
        ]
        return lax.ppermute(value, ("patch", "chan"), pairs)

    made = project_qkv(
        member, tokens, stale_k, stale_v, w_query, w_key, w_value, near, group
    )
    nears = [trade(made[step], step) for step in range(near)]
    stale_far = pack_stale(member, stale_k, stale_v, tuple(range(near, group)))
    kv_far = [trade(stale_far[step - near], step) for step in range(near, group)]
    q_far = [trade(made[step], step) for step in range(near, group)]
    local = attend_local(made[near:group], made[group:])
    locals_ = [local if step == 0 else over_chan(local, step) for step in range(chans)]
    result_size = result_rows(rows // 2)
    near_side = [[beside(value, step) for value in nears] for step in range(1, peers)]
    far_side = [[beside(value, step) for value in kv_far] for step in range(1, peers)]
    stale_at = rows // 2 + rows
    near_own = [(value, stale_at) for value in nears]
    near_rest = [(value, stale_at) for side in near_side for value in side]
    far_own = [(value, 0) for value in kv_far]
    far_rest = [(value, 0) for side in far_side for value in side]

    packets = [[] for _ in range(chans)]
    state = attend(nears, near_own + near_rest, rows, 0, True, partial=True)
    heads = attend(nears, far_own + far_rest, rows, None, False, state=state)
    if group > 2:
        mine = [trade(value, at) for at, value in enumerate(heads)]
        joined = jnp.concatenate(mine, axis=0)
        for step in range(chans):
            value = joined if step == 0 else over_chan(joined, step)
            packets[step] += [(value, at * (rows // 2), None, 0) for at in range(near)]
    else:
        for step in range(chans):
            for at, value in enumerate(heads):
                sent = trade_over_chan(value, at, step)
                packets[step].append((sent, 0, None, 0))
    parts = 2 if group >= 8 else 1
    size = (group - near) // parts
    everything = far_own + near_own + far_rest + near_rest
    for part in range(parts):
        start = part * size
        asked = q_far[start : start + size]
        asked, heads = lax.optimization_barrier((asked, heads))
        heads = attend(asked, everything, rows, start, False, stats=True)
        steps = range(near + start, near + start + size)
        if part < parts - 1:
            mine = [trade(value, at) for at, value in zip(steps, heads)]
            joined = jnp.concatenate(mine, axis=0)
            for step in range(chans):
                value = joined if step == 0 else over_chan(joined, step)
                packets[step] += [
                    (value, at * result_size, locals_[step], (start + at) * result_size)
                    for at in range(size)
                ]
        else:
            for step in range(chans):
                for at, value in zip(steps, heads):
                    sent = trade_over_chan(value, at, step)
                    packets[step].append((sent, 0, locals_[step], (at - near) * result_size))

    share = width // chans
    target = (chan_id + 1) % chans
    scalars = jnp.stack([member[0], target, chan_id])
    resid, gated, part = out_and_ffn(
        scalars, tokens, packets, w_outs, ff_value, ff_gate, ff_down, share
    )
    arrived = [over_chan(part, 1)] if chans > 1 else []
    for step in range(2, chans):
        part = down_project((chan_id + step) % chans, gated, ff_down, share, jnp.bfloat16)
        arrived.append(over_chan(part, step))
    total = down_project(chan_id, gated, ff_down, share, jnp.float32)
    if resid.shape[1] != share:
        resid = lax.dynamic_slice_in_dim(resid, chan_id * share, share, 1)
    total = total + resid
    for part in arrived:
        total = total + part.astype(jnp.float32)
    return total.astype(jnp.bfloat16)


def per_device(
    tokens, stale_k, stale_v, w_query, w_key, w_value, w_out, ff_value, ff_gate, ff_down
):
    chans = lax.axis_size("chan")
    w_outs = [w_out]
    for step in range(1, chans):
        pairs = [(c, (c + step) % chans) for c in range(chans)]
        w_outs.append(lax.ppermute(w_out, "chan", pairs))
    images = [
        image_block(
            tokens[at],
            stale_k[at],
            stale_v[at],
            w_query,
            w_key,
            w_value,
            w_outs,
            ff_value,
            ff_gate,
            ff_down,
        )
        for at in range(tokens.shape[0])
    ]
    return jnp.stack(images)


def solution(mesh):
    return jax.shard_map(
        per_device,
        mesh=mesh,
        in_specs=(
            P(None, "patch", None),
            P(None, "patch", "chan"),
            P(None, "patch", "chan"),
            P(None, "chan"),
            P(None, "chan"),
            P(None, "chan"),
            P("chan", None),
            P(None, "chan"),
            P(None, "chan"),
            P("chan", None),
        ),
        out_specs=P(None, "patch", "chan"),
        check_vma=False,
    )
```

profile of v0, /device:TPU:0, one launch (start us, length us, event | category | flops | bytes accessed | tf_op | source)
XLA Modules:
  0.0 166.4 jit_solution(14575847458579310101)
XLA Ops:
  0.0 8.6 %project_qkv.1 = (bf16[1280,128]{1,0:T(8,128)(2,1)}, bf16[1280,128]{1,0:T(8,128)(2,1)}, bf16[1280,128]{1,0:T(8,128)(2,1)}, bf16[1280,128]{1,0:T(8,128)(2,1)}, bf...) custom-call(s32[1]{0:T(128)} %bitcast.1.member_ref, ...), custom_call_target="tpu_custom_call" | custom-call | flops 2013265920 | bytes 3932160 | tf_op jit(solution)/shard_map/project_qkv/pallas_call | solution.py:250
  8.6 3.1 %collective-permute-start = (bf16[1280,128]{1,0:T(8,128)(2,1)}, bf16[1280,128]{1,0:T(8,128)(2,1)S(1)}, u32[]{:S(2)}, u32[]{:S(2)}) collective-permute-start(bf16[1280,128]{1,0:T(8,128)(2,1)} %get-tuple-element.37), channel_id=1, source_target_pairs={{0,4},{2,6},{4,0},{6,2},{8,12},{10,14},{12,8},{14,10},{16,20},{18,... | collective-permute-start | bytes 983048 | tf_op jit(solution)/shard_map/ppermute | solution.py:580
  14.0 3.0 %collective-permute-start.3 = (bf16[512,128]{1,0:T(8,128)(2,1)S(1)}, bf16[512,128]{1,0:T(8,128)(2,1)S(1)}, u32[]{:S(2)}, u32[]{:S(2)}) collective-permute-start(bf16[512,128]{1,0:T(8,128)(2,1)S(1)} %get-tuple-element.40), channel_id=1, source_target_pairs={{0,16},{2,18},{4,20},{6,22},{8,24},{10,26},{12,28},{14,30},{16,0},... | collective-permute-start | bytes 393224 | tf_op jit(solution)/shard_map/ppermute | solution.py:580
  18.3 13.0 %collective-permute-done.3.refs_4_.refs_2_ = bf16[512,128]{1,0:T(8,128)(2,1)S(1)} collective-permute-done((bf16[512,128]{1,0:T(8,128)(2,1)S(1)}, bf16[512,128]{1,0:T(8,128)(2,1)S(1)}, u32[]{:S(2)}, u32[]{:S(2)}) %collective-permute-start.3) | collective-permute-done | bytes 131104 | tf_op jit(solution)/shard_map/ppermute | solution.py:580
  33.4 3.8 %collective-permute-start.5 = (bf16[512,128]{1,0:T(8,128)(2,1)S(1)}, bf16[512,128]{1,0:T(8,128)(2,1)S(1)}, u32[]{:S(2)}, u32[]{:S(2)}) collective-permute-start(bf16[512,128]{1,0:T(8,128)(2,1)S(1)} %get-tuple-element.42), channel_id=1, source_target_pairs={{0,24},{2,26},{4,28},{6,30},{8,16},{10,18},{12,20},{14,22},{16,8},... | collective-permute-start | bytes 393224 | tf_op jit(solution)/shard_map/ppermute | solution.py:580
  37.2 4.3 %collective-permute-done.5.refs_6_.refs_4_ = bf16[512,128]{1,0:T(8,128)(2,1)S(1)} collective-permute-done((bf16[512,128]{1,0:T(8,128)(2,1)S(1)}, bf16[512,128]{1,0:T(8,128)(2,1)S(1)}, u32[]{:S(2)}, u32[]{:S(2)}) %collective-permute-start.5) | collective-permute-done | bytes 131104 | tf_op jit(solution)/shard_map/ppermute | solution.py:580
  41.5 4.4 %collective-permute-start.6 = (bf16[512,128]{1,0:T(8,128)(2,1)S(1)}, bf16[512,128]{1,0:T(8,128)(2,1)S(1)}, u32[]{:S(2)}, u32[]{:S(2)}) collective-permute-start(bf16[512,128]{1,0:T(8,128)(2,1)S(1)} %get-tuple-element.43), channel_id=1, source_target_pairs={{0,28},{2,30},{4,24},{6,26},{8,20},{10,22},{12,16},{14,18},{16,12}... | collective-permute-start | bytes 393224 | tf_op jit(solution)/shard_map/ppermute | solution.py:580
  45.9 3.7 %attend_local.1.refs_2_ = bf16[1152,128]{1,0:T(8,128)(2,1)S(1)} custom-call(bf16[256,128]{1,0:T(8,128)(2,1)S(1)} %copy-done.8, bf16[256,128]{1,0:T(8,128)(2,1)S(1)} %copy-done.7, bf16[256,128]{1,0:T(8,128)(2,1)S(1)} %copy-done.6, bf16[256,128]{1,0:T(8,128)(2,1)S(1)} %copy-done.5, bf16[512,128]{1,0:T(8,128)(2,1)S(1)} %copy-done.9, ...), custom_call_target="tpu_custom_call" | custom-call | flops 536870912 | bytes 1048576 | tf_op jit(solution)/shard_map/attend_local/pallas_call | solution.py:138
  49.6 3.2 %collective-permute-start.18 = (bf16[256,128]{1,0:T(8,128)(2,1)S(1)}, bf16[256,128]{1,0:T(8,128)(2,1)S(1)}, u32[]{:S(2)}, u32[]{:S(2)}) collective-permute-start(bf16[256,128]{1,0:T(8,128)(2,1)S(1)} %copy-done.8), channel_id=1, source_target_pairs={{0,16},{2,18},{4,20},{6,22},{8,24},{10,26},{12,28},{14,30},{16,0},... | collective-permute-start | bytes 196616 | tf_op jit(solution)/shard_map/ppermute | solution.py:580
  53.9 11.5 %shard_map.100.refs_12_ = f32[4,2,256,128]{3,2,1,0:T(8,128)S(1)} custom-call(bf16[1280,128]{1,0:T(8,128)(2,1)S(1)} %copy-done.3, bf16[1280,128]{1,0:T(8,128)(2,1)S(1)} %collective-permute-done.refs_1_.refs_7_, bf16[1280,128]{1,0:T(8,128)(2,1)S(1)} %collective-permute-done.1.refs_2_.refs_8_, bf16[1280,128]{1,0:T(8,128)(2,1)S(1)} %collective-permute-done.2.refs_3_.refs_9_, ...), custom_call_target="tpu_custom_call" | custom-call | flops 4294967296 | bytes 1048576 | tf_op jit(solution)/shard_map/pallas_call | solution.py:375
  65.8 3.3 %collective-permute-start.22 = (bf16[256,128]{1,0:T(8,128)(2,1)S(1)}, bf16[256,128]{1,0:T(8,128)(2,1)S(1)}, u32[]{:S(2)}, u32[]{:S(2)}) collective-permute-start(bf16[256,128]{1,0:T(8,128)(2,1)S(1)} %copy-done.6), channel_id=1, source_target_pairs={{0,24},{2,26},{4,28},{6,30},{8,16},{10,18},{12,20},{14,22},{16,8},... | collective-permute-start | bytes 196616 | tf_op jit(solution)/shard_map/ppermute | solution.py:580
  71.7 12.1 %shard_map.101 = (bf16[256,128]{1,0:T(8,128)(2,1)S(1)}, bf16[256,128]{1,0:T(8,128)(2,1)S(1)}, bf16[256,128]{1,0:T(8,128)(2,1)S(1)}, bf16[256,128]{1,0:T(8,128)(2,1)S(1)}) custom-call(bf16[1280,128]{1,0:T(8,128)(2,1)S(1)} %copy-done.3, bf16[1280,128]{1,0:T(8,128)(2,1)S(1)} %collective-permute-done.refs_1_.refs_7_, ...), custom_call_target="tpu_custom_call" | custom-call | flops 4294967296 | bytes 1048576 | tf_op jit(solution)/shard_map/pallas_call | solution.py:375
  85.4 10.7 %shard_map.102 = (bf16[288,128]{1,0:T(8,128)(2,1)S(1)}, bf16[288,128]{1,0:T(8,128)(2,1)S(1)}) custom-call(bf16[256,128]{1,0:T(8,128)(2,1)S(1)} %collective-permute-done.18.refs_0_, bf16[256,128]{1,0:T(8,128)(2,1)S(1)} %collective-permute-done.19.refs_1_, bf16[512,128]{1,0:T(8,128)(2,1)S(1)} %collective-permute-done.3.refs_4_.refs_2_, ...), custom_call_target="tpu_custom_call" | custom-call | flops 4294967296 | bytes 2097152 | tf_op jit(solution)/shard_map/pallas_call | solution.py:375
  96.2 2.5 %collective-permute-start.17 = (bf16[256,128]{1,0:T(8,128)(2,1)S(1)}, bf16[256,128]{1,0:T(8,128)(2,1)S(1)}, u32[]{:S(2)}, u32[]{:S(2)}) collective-permute-start(bf16[256,128]{1,0:T(8,128)(2,1)S(1)} %get-tuple-element.47), channel_id=1, source_target_pairs={{0,12},{2,14},{4,8},{6,10},{8,4},{10,6},{12,0},{14,2},{16,28},{18,... | collective-permute-start | bytes 196616 | tf_op jit(solution)/shard_map/ppermute | solution.py:580
  98.7 11.3 %shard_map.103 = (bf16[288,128]{1,0:T(8,128)(2,1)}, bf16[288,128]{1,0:T(8,128)(2,1)S(1)}) custom-call(bf16[256,128]{1,0:T(8,128)(2,1)S(1)} %collective-permute-done.22.refs_0_, bf16[256,128]{1,0:T(8,128)(2,1)S(1)} %collective-permute-done.23.refs_1_, bf16[512,128]{1,0:T(8,128)(2,1)S(1)} %collective-permute-done.3.refs_4_.refs_2_, ...), custom_call_target="tpu_custom_call" | custom-call | flops 4294967296 | bytes 2097152 | tf_op jit(solution)/shard_map/pallas_call | solution.py:375
  111.6 1.8 %collective-permute-start.21 = (bf16[288,128]{1,0:T(8,128)(2,1)S(1)}, bf16[288,128]{1,0:T(8,128)(2,1)S(1)}, u32[]{:S(2)}, u32[]{:S(2)}) collective-permute-start(bf16[288,128]{1,0:T(8,128)(2,1)S(1)} %get-tuple-element.53), channel_id=1, source_target_pairs={{0,20},{2,22},{4,16},{6,18},{8,28},{10,30},{12,24},{14,26},{16,4},... | collective-permute-start | bytes 221192 | tf_op jit(solution)/shard_map/ppermute | solution.py:580
  113.5 4.3 %collective-permute-start.29 = (bf16[288,128]{1,0:T(8,128)(2,1)}, bf16[288,128]{1,0:T(8,128)(2,1)}, u32[]{:S(2)}, u32[]{:S(2)}) collective-permute-start(bf16[288,128]{1,0:T(8,128)(2,1)} %get-tuple-element.62), channel_id=1, source_target_pairs={{0,25},{1,24},{2,27},{3,26},{4,29},{5,28},{6,31},{7,30},{8,17},{9,... | collective-permute-start | bytes 221192 | tf_op jit(solution)/shard_map/ppermute | solution.py:599
  118.2 3.4 %collective-permute-start.26 = (bf16[1024,128]{1,0:T(8,128)(2,1)S(1)}, bf16[1024,128]{1,0:T(8,128)(2,1)}, u32[]{:S(2)}, u32[]{:S(2)}) collective-permute-start(bf16[1024,128]{1,0:T(8,128)(2,1)S(1)} %constant_dynamic-update-slice_fusion.refs_0_), channel_id=1, source_target_pairs={{0,1},{1,0},{2,3},{3,2},{4,5},{5,4},{6,7},{7,6},{8,9},{9,8},{10,11... | collective-permute-start | bytes 786440 | tf_op jit(solution)/shard_map/ppermute | solution.py:589
  123.5 3.1 %collective-permute-start.27 = (bf16[576,128]{1,0:T(8,128)(2,1)S(1)}, bf16[576,128]{1,0:T(8,128)(2,1)S(1)}, u32[]{:S(2)}, u32[]{:S(2)}) collective-permute-start(bf16[576,128]{1,0:T(8,128)(2,1)S(1)} %constant_dynamic-update-slice_fusion.4.refs_1_), channel_id=1, source_target_pairs={{0,1},{1,0},{2,3},{3,2},{4,5},{5,4},{6,7},{7,6},{8,9},{9,8},{10,11... | collective-permute-start | bytes 442376 | tf_op jit(solution)/shard_map/ppermute | solution.py:589
  128.9 2.0 %collective-permute-start.25 = (bf16[288,128]{1,0:T(8,128)(2,1)}, bf16[288,128]{1,0:T(8,128)(2,1)S(1)}, u32[]{:S(2)}, u32[]{:S(2)}) collective-permute-start(bf16[288,128]{1,0:T(8,128)(2,1)} %copy-done.4), channel_id=1, source_target_pairs={{0,28},{2,30},{4,24},{6,26},{8,20},{10,22},{12,16},{14,18},{16,12}... | collective-permute-start | bytes 221192 | tf_op jit(solution)/shard_map/ppermute | solution.py:580
  130.9 3.8 %collective-permute-done.30.refs_9_ = bf16[288,128]{1,0:T(8,128)(2,1)S(1)} collective-permute-done((bf16[288,128]{1,0:T(8,128)(2,1)}, bf16[288,128]{1,0:T(8,128)(2,1)S(1)}, u32[]{:S(2)}, u32[]{:S(2)}) %collective-permute-start.30) | collective-permute-done | bytes 73760 | tf_op jit(solution)/shard_map/ppermute | solution.py:599
  137.5 17.2 %out_and_ffn.1 = (f32[512,640]{1,0:T(8,128)S(1)}, bf16[512,2560]{1,0:T(8,128)(2,1)S(1)}, bf16[512,640]{1,0:T(8,128)(2,1)S(1)}) custom-call(s32[3]{0:T(128)S(1)} %pad_add_fusion.scalars_ref, bf16[512,1280]{1,0:T(8,128)(2,1)S(1)} %bitcast.11, bf16[1024,128]{1,0:T(8,128)(2,1)S(1)} %constant_dynamic-update-slice_fusion.refs_0_, ...), custom_call_target="tpu_custom_call" | custom-call | flops 6710886400 | bytes 13107200 | tf_op jit(solution)/shard_map/out_and_ffn/pallas_call | solution.py:484
  156.3 3.2 %down_project.1 = f32[512,640]{1,0:T(8,128)S(1)} custom-call(s32[1]{0:T(128)} %bitcast.target_ref, bf16[512,2560]{1,0:T(8,128)(2,1)S(1)} %get-tuple-element.64.gated_ref, bf16[2560,1280]{1,0:T(8,128)(2,1)S(1)} %bitcast.9), custom_call_target="tpu_custom_call" | custom-call | flops 1677721600 | bytes 3276800 | tf_op jit(solution)/shard_map/down_project/pallas_call | solution.py:538
  159.5 5.9 %collective-permute-done.32 = bf16[512,640]{1,0:T(8,128)(2,1)S(1)} collective-permute-done((bf16[512,640]{1,0:T(8,128)(2,1)S(1)}, bf16[512,640]{1,0:T(8,128)(2,1)S(1)}, u32[]{:S(2)}, u32[]{:S(2)}) %collective-permute-start.32) | collective-permute-done | bytes 655392 | tf_op jit(solution)/shard_map/ppermute | solution.py:589
  (90 shorter events, 23.0 us)
Async XLA Ops:
  8.6 22.8 %collective-permute-start = (bf16[1280,128]{1,0:T(8,128)(2,1)}, bf16[1280,128]{1,0:T(8,128)(2,1)S(1)}, u32[]{:S(2)}, u32[]{:S(2)}) collective-permute-start(bf16[1280,128]{1,0:T(8,128)(2,1)} %get-tuple-element.37), channel_id=1, source_target_pairs={{0,4},{2,6},{4,0},{6,2},{8,12},{10,14},{12,8},{14,10},{16,20},{18,... | collective-permute-start | bytes 983048 | tf_op jit(solution)/shard_map/ppermute | solution.py:580
  11.6 20.2 %collective-permute-start.1 = (bf16[1280,128]{1,0:T(8,128)(2,1)}, bf16[1280,128]{1,0:T(8,128)(2,1)S(1)}, u32[]{:S(2)}, u32[]{:S(2)}) collective-permute-start(bf16[1280,128]{1,0:T(8,128)(2,1)} %get-tuple-element.38), channel_id=1, source_target_pairs={{0,8},{2,10},{4,12},{6,14},{8,0},{10,2},{12,4},{14,6},{16,24},{18,... | collective-permute-start | bytes 983048 | tf_op jit(solution)/shard_map/ppermute | solution.py:580
  13.3 20.2 %collective-permute-start.2 = (bf16[1280,128]{1,0:T(8,128)(2,1)}, bf16[1280,128]{1,0:T(8,128)(2,1)S(1)}, u32[]{:S(2)}, u32[]{:S(2)}) collective-permute-start(bf16[1280,128]{1,0:T(8,128)(2,1)} %get-tuple-element.39), channel_id=1, source_target_pairs={{0,12},{2,14},{4,8},{6,10},{8,4},{10,6},{12,0},{14,2},{16,28},{18,... | collective-permute-start | bytes 983048 | tf_op jit(solution)/shard_map/ppermute | solution.py:580
  14.0 17.3 %collective-permute-start.3 = (bf16[512,128]{1,0:T(8,128)(2,1)S(1)}, bf16[512,128]{1,0:T(8,128)(2,1)S(1)}, u32[]{:S(2)}, u32[]{:S(2)}) collective-permute-start(bf16[512,128]{1,0:T(8,128)(2,1)S(1)} %get-tuple-element.40), channel_id=1, source_target_pairs={{0,16},{2,18},{4,20},{6,22},{8,24},{10,26},{12,28},{14,30},{16,0},... | collective-permute-start | bytes 393224 | tf_op jit(solution)/shard_map/ppermute | solution.py:580
  17.0 16.4 %collective-permute-start.4 = (bf16[512,128]{1,0:T(8,128)(2,1)S(1)}, bf16[512,128]{1,0:T(8,128)(2,1)S(1)}, u32[]{:S(2)}, u32[]{:S(2)}) collective-permute-start(bf16[512,128]{1,0:T(8,128)(2,1)S(1)} %get-tuple-element.41), channel_id=1, source_target_pairs={{0,20},{2,22},{4,16},{6,18},{8,28},{10,30},{12,24},{14,26},{16,4},... | collective-permute-start | bytes 393224 | tf_op jit(solution)/shard_map/ppermute | solution.py:580
  31.3 21.5 %collective-permute-start.11 = (bf16[1280,128]{1,0:T(8,128)(2,1)S(1)}, bf16[1280,128]{1,0:T(8,128)(2,1)S(1)}, u32[]{:S(2)}, u32[]{:S(2)}) collective-permute-start(bf16[1280,128]{1,0:T(8,128)(2,1)S(1)} %copy-done.3), channel_id=1, source_target_pairs={{0,2},{2,0},{4,6},{6,4},{8,10},{10,8},{12,14},{14,12},{16,18},{18,... | collective-permute-start | bytes 983048 | tf_op jit(solution)/shard_map/ppermute | solution.py:586
  31.4 21.5 %collective-permute-start.12 = (bf16[1280,128]{1,0:T(8,128)(2,1)S(1)}, bf16[1280,128]{1,0:T(8,128)(2,1)S(1)}, u32[]{:S(2)}, u32[]{:S(2)}) collective-permute-start(bf16[1280,128]{1,0:T(8,128)(2,1)S(1)} %collective-permute-done.refs_1_.refs_7_), channel_id=1, source_target_pairs={{0,2},{2,0},{4,6},{6,4},{8,10},{10,8},{12,14},{14,12},{16,18},{18,... | collective-permute-start | bytes 983048 | tf_op jit(solution)/shard_map/ppermute | solution.py:586
  31.9 21.5 %collective-permute-start.13 = (bf16[1280,128]{1,0:T(8,128)(2,1)S(1)}, bf16[1280,128]{1,0:T(8,128)(2,1)S(1)}, u32[]{:S(2)}, u32[]{:S(2)}) collective-permute-start(bf16[1280,128]{1,0:T(8,128)(2,1)S(1)} %collective-permute-done.1.refs_2_.refs_8_), channel_id=1, source_target_pairs={{0,2},{2,0},{4,6},{6,4},{8,10},{10,8},{12,14},{14,12},{16,18},{18,... | collective-permute-start | bytes 983048 | tf_op jit(solution)/shard_map/ppermute | solution.py:586
  33.4 20.0 %collective-permute-start.14 = (bf16[1280,128]{1,0:T(8,128)(2,1)S(1)}, bf16[1280,128]{1,0:T(8,128)(2,1)S(1)}, u32[]{:S(2)}, u32[]{:S(2)}) collective-permute-start(bf16[1280,128]{1,0:T(8,128)(2,1)S(1)} %collective-permute-done.2.refs_3_.refs_9_), channel_id=1, source_target_pairs={{0,2},{2,0},{4,6},{6,4},{8,10},{10,8},{12,14},{14,12},{16,18},{18,... | collective-permute-start | bytes 983048 | tf_op jit(solution)/shard_map/ppermute | solution.py:586
  49.6 34.2 %collective-permute-start.18 = (bf16[256,128]{1,0:T(8,128)(2,1)S(1)}, bf16[256,128]{1,0:T(8,128)(2,1)S(1)}, u32[]{:S(2)}, u32[]{:S(2)}) collective-permute-start(bf16[256,128]{1,0:T(8,128)(2,1)S(1)} %copy-done.8), channel_id=1, source_target_pairs={{0,16},{2,18},{4,20},{6,22},{8,24},{10,26},{12,28},{14,30},{16,0},... | collective-permute-start | bytes 196616 | tf_op jit(solution)/shard_map/ppermute | solution.py:580
  52.8 13.0 %collective-permute-start.8 = (bf16[512,128]{1,0:T(8,128)(2,1)S(1)}, bf16[512,128]{1,0:T(8,128)(2,1)S(1)}, u32[]{:S(2)}, u32[]{:S(2)}) collective-permute-start(bf16[512,128]{1,0:T(8,128)(2,1)S(1)} %collective-permute-done.4.refs_5_.refs_3_), channel_id=1, source_target_pairs={{0,2},{2,0},{4,6},{6,4},{8,10},{10,8},{12,14},{14,12},{16,18},{18,... | collective-permute-start | bytes 393224 | tf_op jit(solution)/shard_map/ppermute | solution.py:586
  53.4 15.8 %collective-permute-start.9 = (bf16[512,128]{1,0:T(8,128)(2,1)S(1)}, bf16[512,128]{1,0:T(8,128)(2,1)S(1)}, u32[]{:S(2)}, u32[]{:S(2)}) collective-permute-start(bf16[512,128]{1,0:T(8,128)(2,1)S(1)} %collective-permute-done.5.refs_6_.refs_4_), channel_id=1, source_target_pairs={{0,2},{2,0},{4,6},{6,4},{8,10},{10,8},{12,14},{14,12},{16,18},{18,... | collective-permute-start | bytes 393224 | tf_op jit(solution)/shard_map/ppermute | solution.py:586
  53.4 16.8 %collective-permute-start.10 = (bf16[512,128]{1,0:T(8,128)(2,1)S(1)}, bf16[512,128]{1,0:T(8,128)(2,1)S(1)}, u32[]{:S(2)}, u32[]{:S(2)}) collective-permute-start(bf16[512,128]{1,0:T(8,128)(2,1)S(1)} %collective-permute-done.6.refs_7_.refs_5_), channel_id=1, source_target_pairs={{0,2},{2,0},{4,6},{6,4},{8,10},{10,8},{12,14},{14,12},{16,18},{18,... | collective-permute-start | bytes 393224 | tf_op jit(solution)/shard_map/ppermute | solution.py:586
  65.4 19.1 %collective-permute-start.19 = (bf16[256,128]{1,0:T(8,128)(2,1)S(1)}, bf16[256,128]{1,0:T(8,128)(2,1)S(1)}, u32[]{:S(2)}, u32[]{:S(2)}) collective-permute-start(bf16[256,128]{1,0:T(8,128)(2,1)S(1)} %copy-done.7), channel_id=1, source_target_pairs={{0,20},{2,22},{4,16},{6,18},{8,28},{10,30},{12,24},{14,26},{16,4},... | collective-permute-start | bytes 196616 | tf_op jit(solution)/shard_map/ppermute | solution.py:580
  65.8 30.2 %collective-permute-start.22 = (bf16[256,128]{1,0:T(8,128)(2,1)S(1)}, bf16[256,128]{1,0:T(8,128)(2,1)S(1)}, u32[]{:S(2)}, u32[]{:S(2)}) collective-permute-start(bf16[256,128]{1,0:T(8,128)(2,1)S(1)} %copy-done.6), channel_id=1, source_target_pairs={{0,24},{2,26},{4,28},{6,30},{8,16},{10,18},{12,20},{14,22},{16,8},... | collective-permute-start | bytes 196616 | tf_op jit(solution)/shard_map/ppermute | solution.py:580
  69.2 27.0 %collective-permute-start.23 = (bf16[256,128]{1,0:T(8,128)(2,1)S(1)}, bf16[256,128]{1,0:T(8,128)(2,1)S(1)}, u32[]{:S(2)}, u32[]{:S(2)}) collective-permute-start(bf16[256,128]{1,0:T(8,128)(2,1)S(1)} %copy-done.5), channel_id=1, source_target_pairs={{0,28},{2,30},{4,24},{6,26},{8,20},{10,22},{12,16},{14,18},{16,12}... | collective-permute-start | bytes 196616 | tf_op jit(solution)/shard_map/ppermute | solution.py:580
  70.2 65.9 %collective-permute-start.31 = (bf16[512,1280]{1,0:T(8,128)(2,1)}, bf16[512,1280]{1,0:T(8,128)(2,1)}, u32[]{:S(2)}, u32[]{:S(2)}) collective-permute-start(bf16[512,1280]{1,0:T(8,128)(2,1)} %refs_10_.1), channel_id=1, source_target_pairs={{0,1},{1,0},{2,3},{3,2},{4,5},{5,4},{6,7},{7,6},{8,9},{9,8},{10,11... | collective-permute-start | bytes 3932168 | tf_op jit(solution)/shard_map/ppermute | solution.py:683
  83.9 39.6 %collective-permute-start.28 = (bf16[1152,128]{1,0:T(8,128)(2,1)S(1)}, bf16[1152,128]{1,0:T(8,128)(2,1)S(1)}, u32[]{:S(2)}, u32[]{:S(2)}) collective-permute-start(bf16[1152,128]{1,0:T(8,128)(2,1)S(1)} %attend_local.1.refs_2_), channel_id=1, source_target_pairs={{0,1},{1,0},{2,3},{3,2},{4,5},{5,4},{6,7},{7,6},{8,9},{9,8},{10,11... | collective-permute-start | bytes 884744 | tf_op jit(solution)/shard_map/ppermute | solution.py:589
  84.5 25.5 %collective-permute-start.15 = (bf16[256,128]{1,0:T(8,128)(2,1)S(1)}, bf16[256,128]{1,0:T(8,128)(2,1)S(1)}, u32[]{:S(2)}, u32[]{:S(2)}) collective-permute-start(bf16[256,128]{1,0:T(8,128)(2,1)S(1)} %get-tuple-element.45), channel_id=1, source_target_pairs={{0,4},{2,6},{4,0},{6,2},{8,12},{10,14},{12,8},{14,10},{16,20},{18,... | collective-permute-start | bytes 196616 | tf_op jit(solution)/shard_map/ppermute | solution.py:580
  96.1 15.5 %collective-permute-start.16 = (bf16[256,128]{1,0:T(8,128)(2,1)S(1)}, bf16[256,128]{1,0:T(8,128)(2,1)S(1)}, u32[]{:S(2)}, u32[]{:S(2)}) collective-permute-start(bf16[256,128]{1,0:T(8,128)(2,1)S(1)} %get-tuple-element.46), channel_id=1, source_target_pairs={{0,8},{2,10},{4,12},{6,14},{8,0},{10,2},{12,4},{14,6},{16,24},{18,... | collective-permute-start | bytes 196616 | tf_op jit(solution)/shard_map/ppermute | solution.py:580
  96.2 17.3 %collective-permute-start.17 = (bf16[256,128]{1,0:T(8,128)(2,1)S(1)}, bf16[256,128]{1,0:T(8,128)(2,1)S(1)}, u32[]{:S(2)}, u32[]{:S(2)}) collective-permute-start(bf16[256,128]{1,0:T(8,128)(2,1)S(1)} %get-tuple-element.47), channel_id=1, source_target_pairs={{0,12},{2,14},{4,8},{6,10},{8,4},{10,6},{12,0},{14,2},{16,28},{18,... | collective-permute-start | bytes 196616 | tf_op jit(solution)/shard_map/ppermute | solution.py:580
  113.5 13.1 %collective-permute-start.29 = (bf16[288,128]{1,0:T(8,128)(2,1)}, bf16[288,128]{1,0:T(8,128)(2,1)}, u32[]{:S(2)}, u32[]{:S(2)}) collective-permute-start(bf16[288,128]{1,0:T(8,128)(2,1)} %get-tuple-element.62), channel_id=1, source_target_pairs={{0,25},{1,24},{2,27},{3,26},{4,29},{5,28},{6,31},{7,30},{8,17},{9,... | collective-permute-start | bytes 221192 | tf_op jit(solution)/shard_map/ppermute | solution.py:599
  118.2 18.0 %collective-permute-start.26 = (bf16[1024,128]{1,0:T(8,128)(2,1)S(1)}, bf16[1024,128]{1,0:T(8,128)(2,1)}, u32[]{:S(2)}, u32[]{:S(2)}) collective-permute-start(bf16[1024,128]{1,0:T(8,128)(2,1)S(1)} %constant_dynamic-update-slice_fusion.refs_0_), channel_id=1, source_target_pairs={{0,1},{1,0},{2,3},{3,2},{4,5},{5,4},{6,7},{7,6},{8,9},{9,8},{10,11... | collective-permute-start | bytes 786440 | tf_op jit(solution)/shard_map/ppermute | solution.py:589
  123.5 12.7 %collective-permute-start.27 = (bf16[576,128]{1,0:T(8,128)(2,1)S(1)}, bf16[576,128]{1,0:T(8,128)(2,1)S(1)}, u32[]{:S(2)}, u32[]{:S(2)}) collective-permute-start(bf16[576,128]{1,0:T(8,128)(2,1)S(1)} %constant_dynamic-update-slice_fusion.4.refs_1_), channel_id=1, source_target_pairs={{0,1},{1,0},{2,3},{3,2},{4,5},{5,4},{6,7},{7,6},{8,9},{9,8},{10,11... | collective-permute-start | bytes 442376 | tf_op jit(solution)/shard_map/ppermute | solution.py:589
  (24 other events, 484.0 us)
where the time goes:
time: 167 us; the launch traced here: 166 us
  Pallas kernels  78.9 us (47%)
  starting transfers between devices  53.1 us (32%)
  waiting for transfers between devices  31.5 us (19%)
    pallas_call x4, Pallas kernels, attend(): pl.pallas_call(functools.partial(attend_kernel, plan), grid=(count,), in_...  45.6 us
    ppermute x18, starting transfers between devices, trade(): lax.ppermute(value, 'patch', [(p, partner(p, step)) for p in range(patche...  35.1 us
    ppermute x18, waiting for transfers between devices, trade(): lax.ppermute(value, 'patch', [(p, partner(p, step)) for p in range(patche...  21.8 us
    pallas_call x1, Pallas kernels, out_and_ffn(): pl.pallas_call(functools.partial(ffn_kernel, spots, (len(arrays), chans),...  17.2 us
    ppermute x4, starting transfers between devices, over_chan(): lax.ppermute(value, 'chan', [(c, (c + step) % chans) for c in range(chans)])  8.77 us
    pallas_call x1, Pallas kernels, project_qkv(): pl.pallas_call(functools.partial(qkv_kernel, near, group), in_specs=[pl.B...  8.55 us
    ppermute x2, starting transfers between devices, trade_over_chan(): return lax.ppermute(value, ('patch', 'chan'), pairs)  6.15 us
    ppermute x4, waiting for transfers between devices, over_chan(): lax.ppermute(value, 'chan', [(c, (c + step) % chans) for c in range(chans)])  5.86 us
  transfers between devices with their start and end apart: 33, of which 9 were waited for; matrix products, arithmetic and copies ran while one was open for 0% of the time, Pallas kernels for 32%

commit v1 on v0

--- a/solution.py
+++ b/solution.py
@@ -384,7 +384,7 @@
             pltpu.VMEM((count, half + kv_rows if fresh else half, LANES), jnp.bfloat16),
             pltpu.VMEM((result_rows(half), LANES), jnp.bfloat16),
         ],
-        compiler_params=params(4 + blocks * kv_rows // 186, dimension_semantics=("arbitrary",)),
+        compiler_params=params(4 + blocks * kv_rows // 218, dimension_semantics=("arbitrary",)),
         cost_estimate=cost(4 * pairs * LANES, 2 * blocks * kv_rows * LANES, pairs),
     )(*arrays, *(state or ()))
 
@@ -442,7 +442,7 @@
         normed_two[...] = layer_norm(resid).astype(jnp.bfloat16)
 
     block = gated_ref.shape[1]
-    piece = 256 if block % 256 == 0 else block
+    piece = block
     for start in range(0, block, piece):
         ff_val = dot_nn(normed_two[...], val_ref[:, start : start + piece])
         gate = dot_nn(normed_two[...], gate_ref[:, start : start + piece])
@@ -616,7 +616,7 @@
     far_own = [(value, 0) for value in kv_far]
     far_rest = [(value, 0) for side in far_side for value in side]
 
-    packets = [[] for _ in range(chans)]
+    packets = [[None] * group for _ in range(chans)]
     state = attend(nears, near_own + near_rest, rows, 0, True, partial=True)
     heads = attend(nears, far_own + far_rest, rows, None, False, state=state)
     if group > 2:
@@ -624,17 +624,17 @@
         joined = jnp.concatenate(mine, axis=0)
         for step in range(chans):
             value = joined if step == 0 else over_chan(joined, step)
-            packets[step] += [(value, at * (rows // 2), None, 0) for at in range(near)]
+            packets[step][:near] = [(value, at * (rows // 2), None, 0) for at in range(near)]
     else:
         for step in range(chans):
             for at, value in enumerate(heads):
                 sent = trade_over_chan(value, at, step)
-                packets[step].append((sent, 0, None, 0))
+                packets[step][at] = (sent, 0, None, 0)
     parts = 2 if group >= 8 else 1
     size = (group - near) // parts
     everything = far_own + near_own + far_rest + near_rest
     for part in range(parts):
-        start = part * size
+        start = (parts - 1 - part) * size
         asked = q_far[start : start + size]
         asked, heads = lax.optimization_barrier((asked, heads))
         heads = attend(asked, everything, rows, start, False, stats=True)
@@ -644,7 +644,7 @@
             joined = jnp.concatenate(mine, axis=0)
             for step in range(chans):
                 value = joined if step == 0 else over_chan(joined, step)
-                packets[step] += [
+                packets[step][near + start : near + start + size] = [
                     (value, at * result_size, locals_[step], (start + at) * result_size)
                     for at in range(size)
                 ]
@@ -652,7 +652,7 @@
             for step in range(chans):
                 for at, value in zip(steps, heads):
                     sent = trade_over_chan(value, at, step)
-                    packets[step].append((sent, 0, locals_[step], (at - near) * result_size))
+                    packets[step][at] = (sent, 0, locals_[step], (at - near) * result_size)
 
     share = width // chans
     target = (chan_id + 1) % chans

time: 167 us -> 169 us (1.012)
  waiting for transfers between devices: 31.5 us -> 37.7 us
  starting transfers between devices: 53.1 us -> 48.6 us
    ppermute x4, waiting for transfers between devices: 5.86 us -> 10.9 us  [over_chan(): lax.ppermute(value, 'chan', [(c, (c + step) % chans) for c in range(chans)])]
    ppermute x2, starting transfers between devices: 6.15 us -> 1.83 us  [trade_over_chan(): return lax.ppermute(value, ('patch', 'chan'), pairs)]
    ppermute x4, starting transfers between devices: 8.77 us -> 5.34 us  [over_chan(): lax.ppermute(value, 'chan', [(c, (c + step) % chans) for c in range(chans)])]
    ppermute x18, starting transfers between devices: 35.1 us -> 38.4 us  [trade(): lax.ppermute(value, 'patch', [(p, partner(p, step)) for p in range(patche...]
where the time goes in v1:
time: 169 us; the launch traced here: 168 us
  Pallas kernels  79.2 us (47%)
  starting transfers between devices  48.6 us (29%)
  waiting for transfers between devices  37.7 us (22%)
    pallas_call x4, Pallas kernels, attend(): pl.pallas_call(functools.partial(attend_kernel, plan), grid=(count,), in_...  45.6 us
    ppermute x18, starting transfers between devices, trade(): lax.ppermute(value, 'patch', [(p, partner(p, step)) for p in range(patche...  38.4 us
    ppermute x18, waiting for transfers between devices, trade(): lax.ppermute(value, 'patch', [(p, partner(p, step)) for p in range(patche...  22.9 us
    pallas_call x1, Pallas kernels, out_and_ffn(): pl.pallas_call(functools.partial(ffn_kernel, spots, (len(arrays), chans),...  17.5 us
    ppermute x4, waiting for transfers between devices, over_chan(): lax.ppermute(value, 'chan', [(c, (c + step) % chans) for c in range(chans)])  10.9 us
    pallas_call x1, Pallas kernels, project_qkv(): pl.pallas_call(functools.partial(qkv_kernel, near, group), in_specs=[pl.B...  8.55 us
    ppermute x4, starting transfers between devices, over_chan(): lax.ppermute(value, 'chan', [(c, (c + step) % chans) for c in range(chans)])  5.34 us
    ppermute x2, waiting for transfers between devices, trade_over_chan(): return lax.ppermute(value, ('patch', 'chan'), pairs)  3.82 us
  transfers between devices with their start and end apart: 33, of which 9 were waited for; matrix products, arithmetic and copies ran while one was open for 0% of the time, Pallas kernels for 32%

profile of v1, /device:TPU:0, one launch (start us, length us, event | category | flops | bytes accessed | tf_op | source)
XLA Modules:
  0.0 168.4 jit_solution(3519653760300436868)
XLA Ops:
  0.0 8.6 %project_qkv.1 = (bf16[1280,128]{1,0:T(8,128)(2,1)}, bf16[1280,128]{1,0:T(8,128)(2,1)}, bf16[1280,128]{1,0:T(8,128)(2,1)}, bf16[1280,128]{1,0:T(8,128)(2,1)}, bf...) custom-call(s32[1]{0:T(128)} %bitcast.1.member_ref, ...), custom_call_target="tpu_custom_call" | custom-call | flops 2013265920 | bytes 3932160 | tf_op jit(solution)/shard_map/project_qkv/pallas_call | solution.py:250
  8.6 3.1 %collective-permute-start = (bf16[1280,128]{1,0:T(8,128)(2,1)}, bf16[1280,128]{1,0:T(8,128)(2,1)S(1)}, u32[]{:S(2)}, u32[]{:S(2)}) collective-permute-start(bf16[1280,128]{1,0:T(8,128)(2,1)} %get-tuple-element.37), channel_id=1, source_target_pairs={{0,4},{2,6},{4,0},{6,2},{8,12},{10,14},{12,8},{14,10},{16,20},{18,... | collective-permute-start | bytes 983048 | tf_op jit(solution)/shard_map/ppermute | solution.py:580
  14.0 3.0 %collective-permute-start.3 = (bf16[512,128]{1,0:T(8,128)(2,1)S(1)}, bf16[512,128]{1,0:T(8,128)(2,1)S(1)}, u32[]{:S(2)}, u32[]{:S(2)}) collective-permute-start(bf16[512,128]{1,0:T(8,128)(2,1)S(1)} %get-tuple-element.40), channel_id=1, source_target_pairs={{0,16},{2,18},{4,20},{6,22},{8,24},{10,26},{12,28},{14,30},{16,0},... | collective-permute-start | bytes 393224 | tf_op jit(solution)/shard_map/ppermute | solution.py:580
  18.3 13.0 %collective-permute-done.3.refs_4_.refs_2_ = bf16[512,128]{1,0:T(8,128)(2,1)S(1)} collective-permute-done((bf16[512,128]{1,0:T(8,128)(2,1)S(1)}, bf16[512,128]{1,0:T(8,128)(2,1)S(1)}, u32[]{:S(2)}, u32[]{:S(2)}) %collective-permute-start.3) | collective-permute-done | bytes 131104 | tf_op jit(solution)/shard_map/ppermute | solution.py:580
  33.4 3.8 %collective-permute-start.5 = (bf16[512,128]{1,0:T(8,128)(2,1)S(1)}, bf16[512,128]{1,0:T(8,128)(2,1)S(1)}, u32[]{:S(2)}, u32[]{:S(2)}) collective-permute-start(bf16[512,128]{1,0:T(8,128)(2,1)S(1)} %get-tuple-element.42), channel_id=1, source_target_pairs={{0,24},{2,26},{4,28},{6,30},{8,16},{10,18},{12,20},{14,22},{16,8},... | collective-permute-start | bytes 393224 | tf_op jit(solution)/shard_map/ppermute | solution.py:580
  37.2 4.3 %collective-permute-done.5.refs_6_.refs_4_ = bf16[512,128]{1,0:T(8,128)(2,1)S(1)} collective-permute-done((bf16[512,128]{1,0:T(8,128)(2,1)S(1)}, bf16[512,128]{1,0:T(8,128)(2,1)S(1)}, u32[]{:S(2)}, u32[]{:S(2)}) %collective-permute-start.5) | collective-permute-done | bytes 131104 | tf_op jit(solution)/shard_map/ppermute | solution.py:580
  41.5 4.4 %collective-permute-start.6 = (bf16[512,128]{1,0:T(8,128)(2,1)S(1)}, bf16[512,128]{1,0:T(8,128)(2,1)S(1)}, u32[]{:S(2)}, u32[]{:S(2)}) collective-permute-start(bf16[512,128]{1,0:T(8,128)(2,1)S(1)} %get-tuple-element.43), channel_id=1, source_target_pairs={{0,28},{2,30},{4,24},{6,26},{8,20},{10,22},{12,16},{14,18},{16,12}... | collective-permute-start | bytes 393224 | tf_op jit(solution)/shard_map/ppermute | solution.py:580
  45.9 3.7 %attend_local.1.refs_2_ = bf16[1152,128]{1,0:T(8,128)(2,1)S(1)} custom-call(bf16[256,128]{1,0:T(8,128)(2,1)S(1)} %copy-done.6, bf16[256,128]{1,0:T(8,128)(2,1)S(1)} %copy-done.5, bf16[256,128]{1,0:T(8,128)(2,1)S(1)} %copy-done.8, bf16[256,128]{1,0:T(8,128)(2,1)S(1)} %copy-done.7, bf16[512,128]{1,0:T(8,128)(2,1)S(1)} %copy-done.9, ...), custom_call_target="tpu_custom_call" | custom-call | flops 536870912 | bytes 1048576 | tf_op jit(solution)/shard_map/attend_local/pallas_call | solution.py:138
  49.6 3.2 %collective-permute-start.18 = (bf16[256,128]{1,0:T(8,128)(2,1)S(1)}, bf16[256,128]{1,0:T(8,128)(2,1)S(1)}, u32[]{:S(2)}, u32[]{:S(2)}) collective-permute-start(bf16[256,128]{1,0:T(8,128)(2,1)S(1)} %copy-done.6), channel_id=1, source_target_pairs={{0,16},{2,18},{4,20},{6,22},{8,24},{10,26},{12,28},{14,30},{16,0},... | collective-permute-start | bytes 196616 | tf_op jit(solution)/shard_map/ppermute | solution.py:580
  53.9 11.5 %shard_map.100.refs_12_ = f32[4,2,256,128]{3,2,1,0:T(8,128)S(1)} custom-call(bf16[1280,128]{1,0:T(8,128)(2,1)S(1)} %copy-done.3, bf16[1280,128]{1,0:T(8,128)(2,1)S(1)} %collective-permute-done.refs_1_.refs_7_, bf16[1280,128]{1,0:T(8,128)(2,1)S(1)} %collective-permute-done.1.refs_2_.refs_8_, bf16[1280,128]{1,0:T(8,128)(2,1)S(1)} %collective-permute-done.2.refs_3_.refs_9_, ...), custom_call_target="tpu_custom_call" | custom-call | flops 4294967296 | bytes 1048576 | tf_op jit(solution)/shard_map/pallas_call | solution.py:375
  65.8 3.3 %collective-permute-start.20 = (bf16[256,128]{1,0:T(8,128)(2,1)S(1)}, bf16[256,128]{1,0:T(8,128)(2,1)S(1)}, u32[]{:S(2)}, u32[]{:S(2)}) collective-permute-start(bf16[256,128]{1,0:T(8,128)(2,1)S(1)} %copy-done.8), channel_id=1, source_target_pairs={{0,24},{2,26},{4,28},{6,30},{8,16},{10,18},{12,20},{14,22},{16,8},... | collective-permute-start | bytes 196616 | tf_op jit(solution)/shard_map/ppermute | solution.py:580
  71.7 12.1 %shard_map.101 = (bf16[256,128]{1,0:T(8,128)(2,1)S(1)}, bf16[256,128]{1,0:T(8,128)(2,1)S(1)}, bf16[256,128]{1,0:T(8,128)(2,1)S(1)}, bf16[256,128]{1,0:T(8,128)(2,1)S(1)}) custom-call(bf16[1280,128]{1,0:T(8,128)(2,1)S(1)} %copy-done.3, bf16[1280,128]{1,0:T(8,128)(2,1)S(1)} %collective-permute-done.refs_1_.refs_7_, ...), custom_call_target="tpu_custom_call" | custom-call | flops 4294967296 | bytes 1048576 | tf_op jit(solution)/shard_map/pallas_call | solution.py:375
  85.4 10.7 %shard_map.102 = (bf16[288,128]{1,0:T(8,128)(2,1)S(1)}, bf16[288,128]{1,0:T(8,128)(2,1)S(1)}) custom-call(bf16[256,128]{1,0:T(8,128)(2,1)S(1)} %collective-permute-done.20.refs_0_, bf16[256,128]{1,0:T(8,128)(2,1)S(1)} %collective-permute-done.21.refs_1_, bf16[512,128]{1,0:T(8,128)(2,1)S(1)} %collective-permute-done.3.refs_4_.refs_2_, ...), custom_call_target="tpu_custom_call" | custom-call | flops 4294967296 | bytes 2097152 | tf_op jit(solution)/shard_map/pallas_call | solution.py:375
  96.2 2.5 %collective-permute-start.17 = (bf16[256,128]{1,0:T(8,128)(2,1)S(1)}, bf16[256,128]{1,0:T(8,128)(2,1)S(1)}, u32[]{:S(2)}, u32[]{:S(2)}) collective-permute-start(bf16[256,128]{1,0:T(8,128)(2,1)S(1)} %get-tuple-element.47), channel_id=1, source_target_pairs={{0,12},{2,14},{4,8},{6,10},{8,4},{10,6},{12,0},{14,2},{16,28},{18,... | collective-permute-start | bytes 196616 | tf_op jit(solution)/shard_map/ppermute | solution.py:580
  98.7 11.3 %shard_map.103 = (bf16[288,128]{1,0:T(8,128)(2,1)}, bf16[288,128]{1,0:T(8,128)(2,1)S(1)}) custom-call(bf16[256,128]{1,0:T(8,128)(2,1)S(1)} %collective-permute-done.18.refs_0_, bf16[256,128]{1,0:T(8,128)(2,1)S(1)} %collective-permute-done.19.refs_1_, bf16[512,128]{1,0:T(8,128)(2,1)S(1)} %collective-permute-done.3.refs_4_.refs_2_, ...), custom_call_target="tpu_custom_call" | custom-call | flops 4294967296 | bytes 2097152 | tf_op jit(solution)/shard_map/pallas_call | solution.py:375
  110.0 3.0 %collective-permute-start.24 = (bf16[288,128]{1,0:T(8,128)(2,1)S(1)}, bf16[288,128]{1,0:T(8,128)(2,1)S(1)}, u32[]{:S(2)}, u32[]{:S(2)}) collective-permute-start(bf16[288,128]{1,0:T(8,128)(2,1)S(1)} %get-tuple-element.54), channel_id=1, source_target_pairs={{0,24},{2,26},{4,28},{6,30},{8,16},{10,18},{12,20},{14,22},{16,8},... | collective-permute-start | bytes 221192 | tf_op jit(solution)/shard_map/ppermute | solution.py:580
  118.3 2.2 %collective-permute-done.25 = bf16[288,128]{1,0:T(8,128)(2,1)S(1)} collective-permute-done((bf16[288,128]{1,0:T(8,128)(2,1)S(1)}, bf16[288,128]{1,0:T(8,128)(2,1)S(1)}, u32[]{:S(2)}, u32[]{:S(2)}) %collective-permute-start.25) | collective-permute-done | bytes 73760 | tf_op jit(solution)/shard_map/ppermute | solution.py:580
  120.4 2.6 %collective-permute-start.22 = (bf16[288,128]{1,0:T(8,128)(2,1)}, bf16[288,128]{1,0:T(8,128)(2,1)}, u32[]{:S(2)}, u32[]{:S(2)}) collective-permute-start(bf16[288,128]{1,0:T(8,128)(2,1)} %get-tuple-element.58), channel_id=1, source_target_pairs={{0,16},{2,18},{4,20},{6,22},{8,24},{10,26},{12,28},{14,30},{16,0},... | collective-permute-start | bytes 221192 | tf_op jit(solution)/shard_map/ppermute | solution.py:580
  123.1 2.0 %collective-permute-start.30 = (bf16[576,128]{1,0:T(8,128)(2,1)S(1)}, bf16[576,128]{1,0:T(8,128)(2,1)S(1)}, u32[]{:S(2)}, u32[]{:S(2)}) collective-permute-start(bf16[576,128]{1,0:T(8,128)(2,1)S(1)} %constant_dynamic-update-slice_fusion.4.refs_4_), channel_id=1, source_target_pairs={{0,1},{1,0},{2,3},{3,2},{4,5},{5,4},{6,7},{7,6},{8,9},{9,8},{10,11... | collective-permute-start | bytes 442376 | tf_op jit(solution)/shard_map/ppermute | solution.py:589
  126.0 2.8 %collective-permute-start.23 = (bf16[288,128]{1,0:T(8,128)(2,1)}, bf16[288,128]{1,0:T(8,128)(2,1)S(1)}, u32[]{:S(2)}, u32[]{:S(2)}) collective-permute-start(bf16[288,128]{1,0:T(8,128)(2,1)} %copy-done.4), channel_id=1, source_target_pairs={{0,20},{2,22},{4,16},{6,18},{8,28},{10,30},{12,24},{14,26},{16,4},... | collective-permute-start | bytes 221192 | tf_op jit(solution)/shard_map/ppermute | solution.py:580
  128.8 3.8 %collective-permute-done.29.refs_8_ = bf16[288,128]{1,0:T(8,128)(2,1)S(1)} collective-permute-done((bf16[288,128]{1,0:T(8,128)(2,1)}, bf16[288,128]{1,0:T(8,128)(2,1)S(1)}, u32[]{:S(2)}, u32[]{:S(2)}) %collective-permute-start.29) | collective-permute-done | bytes 73760 | tf_op jit(solution)/shard_map/ppermute | solution.py:599
  134.5 17.5 %out_and_ffn.1 = (f32[512,640]{1,0:T(8,128)S(1)}, bf16[512,2560]{1,0:T(8,128)(2,1)S(1)}, bf16[512,640]{1,0:T(8,128)(2,1)S(1)}) custom-call(s32[3]{0:T(128)S(1)} %pad_add_fusion.scalars_ref, bf16[512,1280]{1,0:T(8,128)(2,1)S(1)} %bitcast.11, bf16[1024,128]{1,0:T(8,128)(2,1)S(1)} %constant_dynamic-update-slice_fusion.refs_0_, ...), custom_call_target="tpu_custom_call" | custom-call | flops 6710886400 | bytes 13107200 | tf_op jit(solution)/shard_map/out_and_ffn/pallas_call | solution.py:484
  153.2 3.2 %down_project.1 = f32[512,640]{1,0:T(8,128)S(1)} custom-call(s32[1]{0:T(128)} %bitcast.target_ref, bf16[512,2560]{1,0:T(8,128)(2,1)S(1)} %get-tuple-element.64.gated_ref, bf16[2560,1280]{1,0:T(8,128)(2,1)S(1)} %bitcast.9), custom_call_target="tpu_custom_call" | custom-call | flops 1677721600 | bytes 3276800 | tf_op jit(solution)/shard_map/down_project/pallas_call | solution.py:538
  156.4 10.9 %collective-permute-done.32 = bf16[512,640]{1,0:T(8,128)(2,1)S(1)} collective-permute-done((bf16[512,640]{1,0:T(8,128)(2,1)S(1)}, bf16[512,640]{1,0:T(8,128)(2,1)S(1)}, u32[]{:S(2)}, u32[]{:S(2)}) %collective-permute-start.32) | collective-permute-done | bytes 655392 | tf_op jit(solution)/shard_map/ppermute | solution.py:589
  (90 shorter events, 21.9 us)
Async XLA Ops:
  8.6 22.8 %collective-permute-start = (bf16[1280,128]{1,0:T(8,128)(2,1)}, bf16[1280,128]{1,0:T(8,128)(2,1)S(1)}, u32[]{:S(2)}, u32[]{:S(2)}) collective-permute-start(bf16[1280,128]{1,0:T(8,128)(2,1)} %get-tuple-element.37), channel_id=1, source_target_pairs={{0,4},{2,6},{4,0},{6,2},{8,12},{10,14},{12,8},{14,10},{16,20},{18,... | collective-permute-start | bytes 983048 | tf_op jit(solution)/shard_map/ppermute | solution.py:580
  11.6 20.2 %collective-permute-start.1 = (bf16[1280,128]{1,0:T(8,128)(2,1)}, bf16[1280,128]{1,0:T(8,128)(2,1)S(1)}, u32[]{:S(2)}, u32[]{:S(2)}) collective-permute-start(bf16[1280,128]{1,0:T(8,128)(2,1)} %get-tuple-element.38), channel_id=1, source_target_pairs={{0,8},{2,10},{4,12},{6,14},{8,0},{10,2},{12,4},{14,6},{16,24},{18,... | collective-permute-start | bytes 983048 | tf_op jit(solution)/shard_map/ppermute | solution.py:580
  13.3 20.2 %collective-permute-start.2 = (bf16[1280,128]{1,0:T(8,128)(2,1)}, bf16[1280,128]{1,0:T(8,128)(2,1)S(1)}, u32[]{:S(2)}, u32[]{:S(2)}) collective-permute-start(bf16[1280,128]{1,0:T(8,128)(2,1)} %get-tuple-element.39), channel_id=1, source_target_pairs={{0,12},{2,14},{4,8},{6,10},{8,4},{10,6},{12,0},{14,2},{16,28},{18,... | collective-permute-start | bytes 983048 | tf_op jit(solution)/shard_map/ppermute | solution.py:580
  14.0 17.3 %collective-permute-start.3 = (bf16[512,128]{1,0:T(8,128)(2,1)S(1)}, bf16[512,128]{1,0:T(8,128)(2,1)S(1)}, u32[]{:S(2)}, u32[]{:S(2)}) collective-permute-start(bf16[512,128]{1,0:T(8,128)(2,1)S(1)} %get-tuple-element.40), channel_id=1, source_target_pairs={{0,16},{2,18},{4,20},{6,22},{8,24},{10,26},{12,28},{14,30},{16,0},... | collective-permute-start | bytes 393224 | tf_op jit(solution)/shard_map/ppermute | solution.py:580
  17.0 16.4 %collective-permute-start.4 = (bf16[512,128]{1,0:T(8,128)(2,1)S(1)}, bf16[512,128]{1,0:T(8,128)(2,1)S(1)}, u32[]{:S(2)}, u32[]{:S(2)}) collective-permute-start(bf16[512,128]{1,0:T(8,128)(2,1)S(1)} %get-tuple-element.41), channel_id=1, source_target_pairs={{0,20},{2,22},{4,16},{6,18},{8,28},{10,30},{12,24},{14,26},{16,4},... | collective-permute-start | bytes 393224 | tf_op jit(solution)/shard_map/ppermute | solution.py:580
  31.3 21.5 %collective-permute-start.11 = (bf16[1280,128]{1,0:T(8,128)(2,1)S(1)}, bf16[1280,128]{1,0:T(8,128)(2,1)S(1)}, u32[]{:S(2)}, u32[]{:S(2)}) collective-permute-start(bf16[1280,128]{1,0:T(8,128)(2,1)S(1)} %copy-done.3), channel_id=1, source_target_pairs={{0,2},{2,0},{4,6},{6,4},{8,10},{10,8},{12,14},{14,12},{16,18},{18,... | collective-permute-start | bytes 983048 | tf_op jit(solution)/shard_map/ppermute | solution.py:586
  31.4 21.5 %collective-permute-start.12 = (bf16[1280,128]{1,0:T(8,128)(2,1)S(1)}, bf16[1280,128]{1,0:T(8,128)(2,1)S(1)}, u32[]{:S(2)}, u32[]{:S(2)}) collective-permute-start(bf16[1280,128]{1,0:T(8,128)(2,1)S(1)} %collective-permute-done.refs_1_.refs_7_), channel_id=1, source_target_pairs={{0,2},{2,0},{4,6},{6,4},{8,10},{10,8},{12,14},{14,12},{16,18},{18,... | collective-permute-start | bytes 983048 | tf_op jit(solution)/shard_map/ppermute | solution.py:586
  31.9 21.5 %collective-permute-start.13 = (bf16[1280,128]{1,0:T(8,128)(2,1)S(1)}, bf16[1280,128]{1,0:T(8,128)(2,1)S(1)}, u32[]{:S(2)}, u32[]{:S(2)}) collective-permute-start(bf16[1280,128]{1,0:T(8,128)(2,1)S(1)} %collective-permute-done.1.refs_2_.refs_8_), channel_id=1, source_target_pairs={{0,2},{2,0},{4,6},{6,4},{8,10},{10,8},{12,14},{14,12},{16,18},{18,... | collective-permute-start | bytes 983048 | tf_op jit(solution)/shard_map/ppermute | solution.py:586
  33.4 20.0 %collective-permute-start.14 = (bf16[1280,128]{1,0:T(8,128)(2,1)S(1)}, bf16[1280,128]{1,0:T(8,128)(2,1)S(1)}, u32[]{:S(2)}, u32[]{:S(2)}) collective-permute-start(bf16[1280,128]{1,0:T(8,128)(2,1)S(1)} %collective-permute-done.2.refs_3_.refs_9_), channel_id=1, source_target_pairs={{0,2},{2,0},{4,6},{6,4},{8,10},{10,8},{12,14},{14,12},{16,18},{18,... | collective-permute-start | bytes 983048 | tf_op jit(solution)/shard_map/ppermute | solution.py:586
  49.6 46.5 %collective-permute-start.18 = (bf16[256,128]{1,0:T(8,128)(2,1)S(1)}, bf16[256,128]{1,0:T(8,128)(2,1)S(1)}, u32[]{:S(2)}, u32[]{:S(2)}) collective-permute-start(bf16[256,128]{1,0:T(8,128)(2,1)S(1)} %copy-done.6), channel_id=1, source_target_pairs={{0,16},{2,18},{4,20},{6,22},{8,24},{10,26},{12,28},{14,30},{16,0},... | collective-permute-start | bytes 196616 | tf_op jit(solution)/shard_map/ppermute | solution.py:580
  52.8 12.6 %collective-permute-start.7 = (bf16[512,128]{1,0:T(8,128)(2,1)S(1)}, bf16[512,128]{1,0:T(8,128)(2,1)S(1)}, u32[]{:S(2)}, u32[]{:S(2)}) collective-permute-start(bf16[512,128]{1,0:T(8,128)(2,1)S(1)} %collective-permute-done.3.refs_4_.refs_2_), channel_id=1, source_target_pairs={{0,2},{2,0},{4,6},{6,4},{8,10},{10,8},{12,14},{14,12},{16,18},{18,... | collective-permute-start | bytes 393224 | tf_op jit(solution)/shard_map/ppermute | solution.py:586
  52.8 13.0 %collective-permute-start.8 = (bf16[512,128]{1,0:T(8,128)(2,1)S(1)}, bf16[512,128]{1,0:T(8,128)(2,1)S(1)}, u32[]{:S(2)}, u32[]{:S(2)}) collective-permute-start(bf16[512,128]{1,0:T(8,128)(2,1)S(1)} %collective-permute-done.4.refs_5_.refs_3_), channel_id=1, source_target_pairs={{0,2},{2,0},{4,6},{6,4},{8,10},{10,8},{12,14},{14,12},{16,18},{18,... | collective-permute-start | bytes 393224 | tf_op jit(solution)/shard_map/ppermute | solution.py:586
  53.4 15.8 %collective-permute-start.9 = (bf16[512,128]{1,0:T(8,128)(2,1)S(1)}, bf16[512,128]{1,0:T(8,128)(2,1)S(1)}, u32[]{:S(2)}, u32[]{:S(2)}) collective-permute-start(bf16[512,128]{1,0:T(8,128)(2,1)S(1)} %collective-permute-done.5.refs_6_.refs_4_), channel_id=1, source_target_pairs={{0,2},{2,0},{4,6},{6,4},{8,10},{10,8},{12,14},{14,12},{16,18},{18,... | collective-permute-start | bytes 393224 | tf_op jit(solution)/shard_map/ppermute | solution.py:586
  53.4 16.8 %collective-permute-start.10 = (bf16[512,128]{1,0:T(8,128)(2,1)S(1)}, bf16[512,128]{1,0:T(8,128)(2,1)S(1)}, u32[]{:S(2)}, u32[]{:S(2)}) collective-permute-start(bf16[512,128]{1,0:T(8,128)(2,1)S(1)} %collective-permute-done.6.refs_7_.refs_5_), channel_id=1, source_target_pairs={{0,2},{2,0},{4,6},{6,4},{8,10},{10,8},{12,14},{14,12},{16,18},{18,... | collective-permute-start | bytes 393224 | tf_op jit(solution)/shard_map/ppermute | solution.py:586
  65.4 30.8 %collective-permute-start.19 = (bf16[256,128]{1,0:T(8,128)(2,1)S(1)}, bf16[256,128]{1,0:T(8,128)(2,1)S(1)}, u32[]{:S(2)}, u32[]{:S(2)}) collective-permute-start(bf16[256,128]{1,0:T(8,128)(2,1)S(1)} %copy-done.5), channel_id=1, source_target_pairs={{0,20},{2,22},{4,16},{6,18},{8,28},{10,30},{12,24},{14,26},{16,4},... | collective-permute-start | bytes 196616 | tf_op jit(solution)/shard_map/ppermute | solution.py:580
  65.8 18.0 %collective-permute-start.20 = (bf16[256,128]{1,0:T(8,128)(2,1)S(1)}, bf16[256,128]{1,0:T(8,128)(2,1)S(1)}, u32[]{:S(2)}, u32[]{:S(2)}) collective-permute-start(bf16[256,128]{1,0:T(8,128)(2,1)S(1)} %copy-done.8), channel_id=1, source_target_pairs={{0,24},{2,26},{4,28},{6,30},{8,16},{10,18},{12,20},{14,22},{16,8},... | collective-permute-start | bytes 196616 | tf_op jit(solution)/shard_map/ppermute | solution.py:580
  69.2 15.3 %collective-permute-start.21 = (bf16[256,128]{1,0:T(8,128)(2,1)S(1)}, bf16[256,128]{1,0:T(8,128)(2,1)S(1)}, u32[]{:S(2)}, u32[]{:S(2)}) collective-permute-start(bf16[256,128]{1,0:T(8,128)(2,1)S(1)} %copy-done.7), channel_id=1, source_target_pairs={{0,28},{2,30},{4,24},{6,26},{8,20},{10,22},{12,16},{14,18},{16,12}... | collective-permute-start | bytes 196616 | tf_op jit(solution)/shard_map/ppermute | solution.py:580
  70.2 63.0 %collective-permute-start.31 = (bf16[512,1280]{1,0:T(8,128)(2,1)}, bf16[512,1280]{1,0:T(8,128)(2,1)}, u32[]{:S(2)}, u32[]{:S(2)}) collective-permute-start(bf16[512,1280]{1,0:T(8,128)(2,1)} %refs_10_.1), channel_id=1, source_target_pairs={{0,1},{1,0},{2,3},{3,2},{4,5},{5,4},{6,7},{7,6},{8,9},{9,8},{10,11... | collective-permute-start | bytes 3932168 | tf_op jit(solution)/shard_map/ppermute | solution.py:683
  83.9 39.2 %collective-permute-start.28 = (bf16[1152,128]{1,0:T(8,128)(2,1)S(1)}, bf16[1152,128]{1,0:T(8,128)(2,1)S(1)}, u32[]{:S(2)}, u32[]{:S(2)}) collective-permute-start(bf16[1152,128]{1,0:T(8,128)(2,1)S(1)} %attend_local.1.refs_2_), channel_id=1, source_target_pairs={{0,1},{1,0},{2,3},{3,2},{4,5},{5,4},{6,7},{7,6},{8,9},{9,8},{10,11... | collective-permute-start | bytes 884744 | tf_op jit(solution)/shard_map/ppermute | solution.py:589
  84.5 25.6 %collective-permute-start.15 = (bf16[256,128]{1,0:T(8,128)(2,1)S(1)}, bf16[256,128]{1,0:T(8,128)(2,1)S(1)}, u32[]{:S(2)}, u32[]{:S(2)}) collective-permute-start(bf16[256,128]{1,0:T(8,128)(2,1)S(1)} %get-tuple-element.45), channel_id=1, source_target_pairs={{0,4},{2,6},{4,0},{6,2},{8,12},{10,14},{12,8},{14,10},{16,20},{18,... | collective-permute-start | bytes 196616 | tf_op jit(solution)/shard_map/ppermute | solution.py:580
  96.1 16.9 %collective-permute-start.16 = (bf16[256,128]{1,0:T(8,128)(2,1)S(1)}, bf16[256,128]{1,0:T(8,128)(2,1)S(1)}, u32[]{:S(2)}, u32[]{:S(2)}) collective-permute-start(bf16[256,128]{1,0:T(8,128)(2,1)S(1)} %get-tuple-element.46), channel_id=1, source_target_pairs={{0,8},{2,10},{4,12},{6,14},{8,0},{10,2},{12,4},{14,6},{16,24},{18,... | collective-permute-start | bytes 196616 | tf_op jit(solution)/shard_map/ppermute | solution.py:580
  96.2 18.2 %collective-permute-start.17 = (bf16[256,128]{1,0:T(8,128)(2,1)S(1)}, bf16[256,128]{1,0:T(8,128)(2,1)S(1)}, u32[]{:S(2)}, u32[]{:S(2)}) collective-permute-start(bf16[256,128]{1,0:T(8,128)(2,1)S(1)} %get-tuple-element.47), channel_id=1, source_target_pairs={{0,12},{2,14},{4,8},{6,10},{8,4},{10,6},{12,0},{14,2},{16,28},{18,... | collective-permute-start | bytes 196616 | tf_op jit(solution)/shard_map/ppermute | solution.py:580
  116.7 16.4 %collective-permute-start.26 = (bf16[1024,128]{1,0:T(8,128)(2,1)S(1)}, bf16[1024,128]{1,0:T(8,128)(2,1)}, u32[]{:S(2)}, u32[]{:S(2)}) collective-permute-start(bf16[1024,128]{1,0:T(8,128)(2,1)S(1)} %constant_dynamic-update-slice_fusion.refs_0_), channel_id=1, source_target_pairs={{0,1},{1,0},{2,3},{3,2},{4,5},{5,4},{6,7},{7,6},{8,9},{9,8},{10,11... | collective-permute-start | bytes 786440 | tf_op jit(solution)/shard_map/ppermute | solution.py:589
  152.0 15.3 %collective-permute-start.32 = (bf16[512,640]{1,0:T(8,128)(2,1)S(1)}, bf16[512,640]{1,0:T(8,128)(2,1)S(1)}, u32[]{:S(2)}, u32[]{:S(2)}) collective-permute-start(bf16[512,640]{1,0:T(8,128)(2,1)S(1)} %get-tuple-element.66), channel_id=1, source_target_pairs={{0,1},{1,0},{2,3},{3,2},{4,5},{5,4},{6,7},{7,6},{8,9},{9,8},{10,11... | collective-permute-start | bytes 1966088 | tf_op jit(solution)/shard_map/ppermute | solution.py:589
  (24 other events, 470.8 us)
